TPU v7x, 32 devices: a whole 2x2x4 slice. The times are simulated.
32 devices in a mesh: dp: 8 (over z, y), group: 4 (over x, core).
Axes of the slice: x: 2, y: 2, z: 4, core: 2. Of those that a mesh axis runs over, the one named last changes fastest.
Arguments:
- keys: int32 [16384], P(('dp', 'group')), may hold values from 0 to 1073741823
- cut: int32 [1], replicated, may hold values from 256 to 1023
- owner: int32 [16384, 1], P(('dp', 'group')), may hold values from 0 to 7; in each aligned block of 512 rows (0 to 511, 512 to 1023, ...) at most 128 rows name the same one
- tokens: int32 [16384, 2048], P(('dp', 'group')), may hold values from 0 to 128255
Outputs:
- histogram: int32 [4096], replicated
- packed_rows: int32 [32768, 2048], P(('dp', 'group'))
- packed_weights: float32 [32768], P(('dp', 'group'))
Inputs may be any that keep to these rules, and one draw needn't show every extreme that they name: Among the examples of one device, at most 128 have the same owner, and some owner has exactly 128.
All inputs are finite; a program needn't handle non-finite values.
Results may differ from a plain program's by a relative error of at most 0.0003.
Values sent between devices are 32-bit elements; how exact they have to be, the bound alone decides.
A program may use at most 128 MiB of HBM per device.

v0:
```python
import jax
import jax.numpy as jnp
from jax import lax
from jax.sharding import PartitionSpec as P

BINS = 4096
BIN_WIDTH = 262144


def body(keys, cut, owner, tokens):
    examples = keys.shape[0]
    width = tokens.shape[1]
    n_owner = lax.axis_size("dp")
    n_member = lax.axis_size("group")
    slots = 2 * examples // (n_owner * n_member)
    capacity = 2 * examples
    bins_of = keys // BIN_WIDTH
    local_hist = jnp.zeros((BINS,), jnp.float32).at[bins_of].add(1.0)
    kept = bins_of >= cut[0]
    dest = owner[:, 0]
    onehot = (
        (dest[:, None] == jnp.arange(n_owner, dtype=jnp.int32)[None, :]) & kept[:, None]
    ).astype(jnp.int32)
    counts = jnp.sum(onehot, axis=0).astype(jnp.float32)
    table = lax.all_gather(counts[None, :], ("dp", "group"), axis=0, tiled=True)
    position = lax.axis_index(("dp", "group"))
    below = jnp.arange(table.shape[0], dtype=jnp.int32) < position
    before = jnp.sum(jnp.where(below[:, None], table, 0.0), axis=0)
    hist = lax.psum(local_hist, ("dp", "group"))
    running = jnp.cumsum(onehot, axis=0) - onehot
    local_rank = jnp.sum(running * onehot, axis=1)
    offset = jnp.sum(before.astype(jnp.int32)[None, :] * onehot, axis=1)
    rank = offset + local_rank
    member = rank % n_member
    outside = n_owner * n_member * slots
    position_send = jnp.where(
        kept, (dest * n_member + member) * slots + local_rank // n_member, outside
    )
    send_rows = jnp.zeros((outside, width), jnp.int32).at[position_send].set(tokens, mode="drop")
    details = jnp.stack([rank // n_member, keys], axis=1)
    send_meta = jnp.full((outside, 2), -1, jnp.int32).at[position_send].set(details, mode="drop")
    send_rows = send_rows.reshape(n_owner, n_member, slots, width)
    send_meta = send_meta.reshape(n_owner, n_member, slots, 2)
    got_rows, got_meta = (
        lax.all_to_all(
            lax.all_to_all(send_rows, "dp", split_axis=0, concat_axis=0, tiled=True),
            "group",
            split_axis=1,
            concat_axis=1,
            tiled=True,
        ),
        lax.all_to_all(
            lax.all_to_all(send_meta, "dp", split_axis=0, concat_axis=0, tiled=True),
            "group",
            split_axis=1,
            concat_axis=1,
            tiled=True,
        ),
    )
    got_rows = got_rows.reshape(-1, width)
    got_meta = got_meta.reshape(-1, 2)
    slot = got_meta[:, 0]
    valid = slot >= 0
    target = jnp.where(valid, slot, capacity)
    suffix = jnp.cumsum(hist[::-1])[::-1]
    total = jnp.maximum(suffix[cut[0]], 1.0)
    got_bins = jnp.clip(got_meta[:, 1] // BIN_WIDTH, 0, BINS - 1)
    weight = jnp.where(valid, suffix[got_bins] / total, 0.0)
    packed_rows = jnp.zeros((capacity, width), jnp.int32).at[target].set(got_rows, mode="drop")
    packed_weights = jnp.zeros((capacity,), jnp.float32).at[target].set(weight, mode="drop")
    return (hist.astype(jnp.int32), packed_rows, packed_weights)


def solution(mesh):
    placed = (P(("dp", "group")), P(), P(("dp", "group"), None), P(("dp", "group"), None))
    return jax.shard_map(
        body,
        mesh=mesh,
        in_specs=placed,
        out_specs=(P(), P(("dp", "group"), None), P(("dp", "group"))),
        check_vma=False,
    )
```

profile of v0, /device:TPU:0, one launch (start us, length us, event | category | flops | bytes accessed | tf_op | source)
XLA Modules:
  0.0 387.2 jit_solution(11714940786831163853)
XLA Ops:
  1.3 0.7 broadcast_compare_fusion
  2.0 0.8 convert_reduce_fusion
  2.8 3.3 scatter_custom_fusion
  6.1 0.1 convert_dynamic-update-slice_fusion
  6.2 42.1 %all-reduce.1 = (f32[4096]{0:T(1024)S(1)}, f32[256]{0:T(256)S(1)}) all-reduce(f32[4096]{0:T(1024)S(1)} %scatter_custom_fusion, f32[256]{0:T(256)S(1)} %convert_dynamic-update-slice_fusion), channel_id=1, replica_groups=mesh['dp'=8,'group'=4] {'dp','group'}, use_global_device_ids=true, to_apply=%region_1.2 | all-reduce | flops 4352 | bytes 34816 | tf_op jit(solution)/shard_map/psum | solution.py:29
  48.3 0.1 reshape.184
  48.4 0.1 select_reduce_fusion.1
  48.5 0.7 fusion.10
  49.2 1.1 reduce-window.15
  50.3 0.2 slice_reduce_fusion.1
  50.6 0.8 select_reduce_fusion
  51.4 0.7 compare_select_fusion.6
  52.1 0.7 pad_add_fusion
  52.8 0.1 copy.19
  52.9 1.8 scatter_custom_fusion.1
  54.8 0.3 copy.20
  55.0 0.7 reshape.203
  55.7 5.3 %all-to-all-start = ((s32[8,1,256]{2,1,0:T(1,128)}), s32[8,1,256]{2,1,0:T(1,128)S(1)}, u32[]{:S(2)}, u32[]{:S(2)}) async-start(s32[8,1,256]{2,1,0:T(1,128)} %reshape.203), calls=%async_computation | async-start | bytes 16384 | tf_op jit(solution)/shard_map/all_to_all | solution.py:53
  61.1 8.6 %scatter_custom_fusion.2 = s32[1024,2048]{1,0:T(8,128)} fusion(s32[512]{0:T(512)S(1)} %get-tuple-element.7, s32[512,2048]{1,0:T(8,128)} %param.7, s32[]{:T(128)} %constant.83.clone.1), kind=kCustom, calls=%fused_computation.8 | custom fusion | bytes 8389120 | tf_op jit(solution)/shard_map/scatter | solution.py:39
  69.7 0.0 all-to-all-done
  69.7 6.0 %all-to-all-start.2 = ((s32[8,4,32,2048]{3,2,1,0:T(8,128)}), s32[8,4,32,2048]{3,2,1,0:T(8,128)}, u32[]{:S(2)}, u32[]{:S(2)}) async-start(s32[8,4,32,2048]{3,2,1,0:T(8,128)} %bitcast.35), calls=%async_computation.2 | async-start | bytes 16777216 | tf_op jit(solution)/shard_map/all_to_all | solution.py:46
  75.7 0.5 broadcast.157
  76.2 0.6 reduce.6
  76.8 0.1 reshape.204
  76.9 0.7 reshape.205
  77.5 179.0 %all-to-all-done.2 = s32[8,4,32,2048]{3,2,1,0:T(8,128)} async-done(((s32[8,4,32,2048]{3,2,1,0:T(8,128)}), s32[8,4,32,2048]{3,2,1,0:T(8,128)}, u32[]{:S(2)}, u32[]{:S(2)}) %all-to-all-start.2) | async-done | bytes 8388640 | tf_op jit(solution)/shard_map/all_to_all | solution.py:46
  256.5 3.2 all-to-all-start.1
  259.8 7.9 %copy.23 = s32[8,4,32,2048]{3,2,0,1:T(8,128)} copy(s32[8,4,32,2048]{3,2,1,0:T(8,128)} %all-to-all-done.2) | data formatting | bytes 16777216 | tf_op jit(solution)/shard_map/all_to_all | solution.py:46
  267.7 0.0 all-to-all-done.1
  267.7 5.7 %all-to-all-start.3 = ((s32[8,4,32,2048]{3,2,0,1:T(8,128)}), s32[8,4,32,2048]{3,2,0,1:T(8,128)}, u32[]{:S(2)}, u32[]{:S(2)}) async-start(s32[8,4,32,2048]{3,2,0,1:T(8,128)} %copy.23), calls=%async_computation.3 | async-start | bytes 16777216 | tf_op jit(solution)/shard_map/all_to_all | solution.py:45
  273.4 0.1 rev.6
  273.4 0.6 convert_element_type.30
  274.0 0.3 reduce-window.19
  274.3 0.1 slice.29
  274.4 0.1 reduce-window.24
  274.5 0.1 slice_reduce_fusion
  274.6 0.1 add_bitcast_fusion
  274.7 0.1 rev.7
  274.7 0.6 dynamic_slice.3
  276.0 0.6 reduce.7
  276.6 0.1 reshape.206
  276.7 0.1 reshape.131
  276.8 6.2 %gather_fusion = f32[1024]{0:T(1024)S(1)} fusion(f32[4096]{0:T(1024)S(1)} %rev.7, s32[1024]{0:T(1024)S(1)} %broadcast_clamp_fusion), kind=kCustom, calls=%fused_computation | custom fusion | bytes 12288 | tf_op jit(solution)/shard_map/gather | solution.py:68
  283.0 4.9 %scatter_custom_fusion.4 = f32[1024]{0:T(1024)} fusion(s32[1024]{0:T(1024)S(1)} %bitcast.51, f32[1024]{0:T(1024)S(1)} %divide_select_fusion, f32[]{:T(128)} %constant.81.clone.1), kind=kCustom, calls=%fused_computation.63 | custom fusion | bytes 4100 | tf_op jit(solution)/shard_map/scatter | solution.py:70
  287.9 78.6 %all-to-all-done.3 = s32[8,4,32,2048]{3,2,0,1:T(8,128)} async-done(((s32[8,4,32,2048]{3,2,0,1:T(8,128)}), s32[8,4,32,2048]{3,2,0,1:T(8,128)}, u32[]{:S(2)}, u32[]{:S(2)}) %all-to-all-start.3) | async-done | bytes 8388640 | tf_op jit(solution)/shard_map/all_to_all | solution.py:45
  366.5 7.7 %copy.24 = s32[8,4,32,2048]{3,2,1,0:T(8,128)} copy(s32[8,4,32,2048]{3,2,0,1:T(8,128)} %all-to-all-done.3) | data formatting | bytes 16777216 | tf_op jit(solution)/shard_map/all_to_all | solution.py:45
  374.2 13.0 %scatter_custom_fusion.3 = s32[1024,2048]{1,0:T(8,128)} fusion(s32[1024]{0:T(1024)S(1)} %bitcast.52, s32[1024,2048]{1,0:T(8,128)} %bitcast.36, s32[]{:T(128)} %constant.83.clone.1), kind=kCustom, calls=%fused_computation.6 | custom fusion | bytes 8389120 | tf_op jit(solution)/shard_map/scatter | solution.py:69
  (14 shorter events, 0.2 us)
Async XLA Ops:
  55.7 13.9 %all-to-all-start = ((s32[8,1,256]{2,1,0:T(1,128)}), s32[8,1,256]{2,1,0:T(1,128)S(1)}, u32[]{:S(2)}, u32[]{:S(2)}) async-start(s32[8,1,256]{2,1,0:T(1,128)} %reshape.203), calls=%async_computation | async-start | bytes 16384 | tf_op jit(solution)/shard_map/all_to_all | solution.py:53
  69.7 186.9 %all-to-all-start.2 = ((s32[8,4,32,2048]{3,2,1,0:T(8,128)}), s32[8,4,32,2048]{3,2,1,0:T(8,128)}, u32[]{:S(2)}, u32[]{:S(2)}) async-start(s32[8,4,32,2048]{3,2,1,0:T(8,128)} %bitcast.35), calls=%async_computation.2 | async-start | bytes 16777216 | tf_op jit(solution)/shard_map/all_to_all | solution.py:46
  256.5 11.1 %all-to-all-start.1 = ((s32[4,1,512]{2,1,0:T(1,128)}), s32[4,1,512]{2,1,0:T(1,128)S(1)}, u32[]{:S(2)}, u32[]{:S(2)}) async-start(s32[4,1,512]{2,1,0:T(1,128)} %reshape.205), calls=%async_computation.1 | async-start | bytes 16384 | tf_op jit(solution)/shard_map/all_to_all | solution.py:52
  267.7 98.8 %all-to-all-start.3 = ((s32[8,4,32,2048]{3,2,0,1:T(8,128)}), s32[8,4,32,2048]{3,2,0,1:T(8,128)}, u32[]{:S(2)}, u32[]{:S(2)}) async-start(s32[8,4,32,2048]{3,2,0,1:T(8,128)} %copy.23), calls=%async_computation.3 | async-start | bytes 16777216 | tf_op jit(solution)/shard_map/all_to_all | solution.py:45
where the time goes:
time: 388 us; the launch traced here: 387 us
  waiting for transfers between devices  258 us (66%)
  local copies, waits for them, and re-layouts  53.9 us (14%)
  blocking collectives  42.1 us (11%)
  starting transfers between devices  20.2 us (5%)
  other arithmetic  11.3 us (3%)
    all_to_all x1, waiting for transfers between devices, body(): lax.all_to_all(send_rows, 'dp', split_axis=0, concat_axis=0, tiled=True)  179 us
    all_to_all x1, waiting for transfers between devices, body(): lax.all_to_all(lax.all_to_all(send_rows, 'dp', split_axis=0, concat_axis=...  78.6 us
    psum x1, blocking collectives, body(): hist = lax.psum(local_hist, ('dp', 'group'))  42.1 us
    scatter x1, local copies, waits for them, and re-layouts, body(): jnp.zeros((capacity, width), jnp.int32).at[target]  13 us
    scatter x1, local copies, waits for them, and re-layouts, body(): jnp.zeros((outside, width), jnp.int32).at[position_send]  8.6 us
    all_to_all x1, local copies, waits for them, and re-layouts, body(): lax.all_to_all(send_rows, 'dp', split_axis=0, concat_axis=0, tiled=True)  7.89 us
  transfers between devices with their start and end apart: 4, of which 2 were waited for; matrix products, arithmetic and copies ran while one was open for 8% of the time, Pallas kernels for 0%

commit v1 on v0

--- a/solution.py
+++ b/solution.py
@@ -26,7 +26,11 @@
     position = lax.axis_index(("dp", "group"))
     below = jnp.arange(table.shape[0], dtype=jnp.int32) < position
     before = jnp.sum(jnp.where(below[:, None], table, 0.0), axis=0)
-    hist = lax.psum(local_hist, ("dp", "group"))
+
+    def hold_the_modes(payload):
+        return lax.psum(lax.psum(payload, "group"), "dp")
+
+    hist = hold_the_modes(local_hist)
     running = jnp.cumsum(onehot, axis=0) - onehot
     local_rank = jnp.sum(running * onehot, axis=1)
     offset = jnp.sum(before.astype(jnp.int32)[None, :] * onehot, axis=1)

time: 388 us -> 440 us (1.13)
  blocking collectives: 42.1 us -> 173 us
  waiting for transfers between devices: 258 us -> 179 us
    psum x1 -> x2, blocking collectives: 42.1 us -> 131 us  [hold_the_modes(): return lax.psum(lax.psum(payload, 'group'), 'dp')]
    all_to_all x1, waiting for transfers between devices: 78.6 us -> 0.01 us  [body(): lax.all_to_all(lax.all_to_all(send_rows, 'dp', split_axis=0, concat_axis=...]
    unnamed x0 -> x1, blocking collectives: none -> 41.9 us
  transfers between devices with their start and end apart: 4 -> 4, of which waited for: 2 -> 1; matrix products, arithmetic and copies ran while one was open for 8% -> 8% of each run, Pallas kernels for 0% -> 0%
where the time goes in v1:
time: 440 us; the launch traced here: 439 us
  waiting for transfers between devices  179 us (41%)
  blocking collectives  173 us (39%)
  local copies, waits for them, and re-layouts  53.9 us (12%)
  starting transfers between devices  20.2 us (5%)
  other arithmetic  11.3 us (3%)
    all_to_all x1, waiting for transfers between devices, body(): lax.all_to_all(send_rows, 'dp', split_axis=0, concat_axis=0, tiled=True)  179 us
    psum x2, blocking collectives, hold_the_modes(): return lax.psum(lax.psum(payload, 'group'), 'dp')  131 us
    unnamed x1, blocking collectives  41.9 us
    scatter x1, local copies, waits for them, and re-layouts, body(): jnp.zeros((capacity, width), jnp.int32).at[target]  13 us
  transfers between devices with their start and end apart: 4, of which 1 were waited for; matrix products, arithmetic and copies ran while one was open for 8% of the time, Pallas kernels for 0%

profile of v1, /device:TPU:0, one launch (start us, length us, event | category | flops | bytes accessed | tf_op | source)
XLA Modules:
  0.0 439.3 jit_solution(8992049857521741574)
XLA Ops:
  1.3 0.7 broadcast_compare_fusion
  2.0 0.8 convert_reduce_fusion
  2.8 0.1 convert_dynamic-update-slice_fusion
  2.9 41.9 %all-reduce = f32[256]{0:T(256)S(1)} all-reduce(f32[256]{0:T(256)S(1)} %convert_dynamic-update-slice_fusion), channel_id=2, replica_groups=mesh['dp'=8,'group'=4] {'dp','group'}, use_global_device_ids=true, to_apply=%add | all-reduce | flops 256 | bytes 2048
  44.8 0.1 reshape.184
  44.9 0.1 select_reduce_fusion.1
  45.0 0.7 fusion.10
  45.7 1.1 reduce-window.15
  46.8 0.2 slice_reduce_fusion.1
  47.1 0.8 select_reduce_fusion
  47.9 0.7 compare_select_fusion.6
  48.6 0.7 pad_add_fusion
  49.3 0.1 copy.19
  49.4 1.8 scatter_custom_fusion.1
  51.3 0.3 copy.20
  51.5 0.7 reshape.203
  52.3 5.3 %all-to-all-start = ((s32[8,1,256]{2,1,0:T(1,128)}), s32[8,1,256]{2,1,0:T(1,128)S(1)}, u32[]{:S(2)}, u32[]{:S(2)}) async-start(s32[8,1,256]{2,1,0:T(1,128)} %reshape.203), calls=%async_computation | async-start | bytes 16384 | tf_op jit(solution)/shard_map/all_to_all | solution.py:57
  57.6 8.6 %scatter_custom_fusion.2 = s32[1024,2048]{1,0:T(8,128)} fusion(s32[512]{0:T(512)S(1)} %get-tuple-element.5, s32[512,2048]{1,0:T(8,128)} %param.7, s32[]{:T(128)} %constant.83.clone.1), kind=kCustom, calls=%fused_computation.8 | custom fusion | bytes 8389120 | tf_op jit(solution)/shard_map/scatter | solution.py:43
  66.2 0.0 all-to-all-done
  66.2 6.0 %all-to-all-start.2 = ((s32[8,4,32,2048]{3,2,1,0:T(8,128)}), s32[8,4,32,2048]{3,2,1,0:T(8,128)}, u32[]{:S(2)}, u32[]{:S(2)}) async-start(s32[8,4,32,2048]{3,2,1,0:T(8,128)} %bitcast.31), calls=%async_computation.2 | async-start | bytes 16777216 | tf_op jit(solution)/shard_map/all_to_all | solution.py:50
  72.2 0.5 broadcast.157
  72.6 0.6 reduce.6
  73.2 0.1 reshape.204
  73.3 0.7 reshape.205
  74.0 179.0 %all-to-all-done.2 = s32[8,4,32,2048]{3,2,1,0:T(8,128)} async-done(((s32[8,4,32,2048]{3,2,1,0:T(8,128)}), s32[8,4,32,2048]{3,2,1,0:T(8,128)}, u32[]{:S(2)}, u32[]{:S(2)}) %all-to-all-start.2) | async-done | bytes 8388640 | tf_op jit(solution)/shard_map/all_to_all | solution.py:50
  253.0 3.2 all-to-all-start.1
  256.3 7.9 %copy.23 = s32[8,4,32,2048]{3,2,0,1:T(8,128)} copy(s32[8,4,32,2048]{3,2,1,0:T(8,128)} %all-to-all-done.2) | data formatting | bytes 16777216 | tf_op jit(solution)/shard_map/all_to_all | solution.py:50
  264.2 5.7 %all-to-all-start.3 = ((s32[8,4,32,2048]{3,2,0,1:T(8,128)}), s32[8,4,32,2048]{3,2,0,1:T(8,128)}, u32[]{:S(2)}, u32[]{:S(2)}) async-start(s32[8,4,32,2048]{3,2,0,1:T(8,128)} %copy.23), calls=%async_computation.3 | async-start | bytes 16777216 | tf_op jit(solution)/shard_map/all_to_all | solution.py:49
  269.9 3.3 scatter_custom_fusion
  273.1 95.6 %psum.14 = f32[4096]{0:T(1024)S(1)} all-reduce(f32[4096]{0:T(1024)S(1)} %scatter_custom_fusion), channel_id=1, replica_groups=mesh['dp'=8,'group'=4] {'group'}, use_global_device_ids=true, to_apply=%region_1.2 | all-reduce | flops 4096 | bytes 32768 | tf_op jit(solution)/shard_map/psum | solution.py:31
  368.8 35.2 %psum.15 = f32[4096]{0:T(1024)S(1)} all-reduce(f32[4096]{0:T(1024)S(1)} %psum.14), channel_id=1, replica_groups=mesh['dp'=8,'group'=4] {'dp'}, use_global_device_ids=true, to_apply=%region_2.3 | all-reduce | flops 4096 | bytes 32768 | tf_op jit(solution)/shard_map/psum | solution.py:31
  404.0 0.1 rev.6
  404.0 0.6 convert_element_type.30
  404.6 0.3 reduce-window.19
  404.9 0.1 slice.29
  405.0 0.1 reduce-window.24
  405.1 0.1 slice_reduce_fusion
  405.2 0.1 add_bitcast_fusion
  405.2 0.1 rev.7
  405.3 0.6 dynamic_slice.3
  406.6 0.6 reduce.7
  407.2 0.1 reshape.206
  407.3 0.1 reshape.131
  407.4 6.2 %gather_fusion = f32[1024]{0:T(1024)S(1)} fusion(f32[4096]{0:T(1024)S(1)} %rev.7, s32[1024]{0:T(1024)S(1)} %broadcast_clamp_fusion), kind=kCustom, calls=%fused_computation | custom fusion | bytes 12288 | tf_op jit(solution)/shard_map/gather | solution.py:72
  413.6 4.9 %scatter_custom_fusion.4 = f32[1024]{0:T(1024)} fusion(s32[1024]{0:T(1024)S(1)} %bitcast.47, f32[1024]{0:T(1024)S(1)} %divide_select_fusion, f32[]{:T(128)} %constant.81.clone.1), kind=kCustom, calls=%fused_computation.63 | custom fusion | bytes 4100 | tf_op jit(solution)/shard_map/scatter | solution.py:74
  418.5 0.0 all-to-all-done.3
  418.5 7.7 %copy.24 = s32[8,4,32,2048]{3,2,1,0:T(8,128)} copy(s32[8,4,32,2048]{3,2,0,1:T(8,128)} %all-to-all-done.3) | data formatting | bytes 16777216 | tf_op jit(solution)/shard_map/all_to_all | solution.py:49
  426.2 13.0 %scatter_custom_fusion.3 = s32[1024,2048]{1,0:T(8,128)} fusion(s32[1024]{0:T(1024)S(1)} %bitcast.48, s32[1024,2048]{1,0:T(8,128)} %bitcast.32, s32[]{:T(128)} %constant.83.clone.1), kind=kCustom, calls=%fused_computation.6 | custom fusion | bytes 8389120 | tf_op jit(solution)/shard_map/scatter | solution.py:73
  (15 shorter events, 0.2 us)
Async XLA Ops:
  52.3 13.9 %all-to-all-start = ((s32[8,1,256]{2,1,0:T(1,128)}), s32[8,1,256]{2,1,0:T(1,128)S(1)}, u32[]{:S(2)}, u32[]{:S(2)}) async-start(s32[8,1,256]{2,1,0:T(1,128)} %reshape.203), calls=%async_computation | async-start | bytes 16384 | tf_op jit(solution)/shard_map/all_to_all | solution.py:57
  66.2 186.9 %all-to-all-start.2 = ((s32[8,4,32,2048]{3,2,1,0:T(8,128)}), s32[8,4,32,2048]{3,2,1,0:T(8,128)}, u32[]{:S(2)}, u32[]{:S(2)}) async-start(s32[8,4,32,2048]{3,2,1,0:T(8,128)} %bitcast.31), calls=%async_computation.2 | async-start | bytes 16777216 | tf_op jit(solution)/shard_map/all_to_all | solution.py:50
  253.0 11.1 %all-to-all-start.1 = ((s32[4,1,512]{2,1,0:T(1,128)}), s32[4,1,512]{2,1,0:T(1,128)S(1)}, u32[]{:S(2)}, u32[]{:S(2)}) async-start(s32[4,1,512]{2,1,0:T(1,128)} %reshape.205), calls=%async_computation.1 | async-start | bytes 16384 | tf_op jit(solution)/shard_map/all_to_all | solution.py:56
  264.2 154.3 %all-to-all-start.3 = ((s32[8,4,32,2048]{3,2,0,1:T(8,128)}), s32[8,4,32,2048]{3,2,0,1:T(8,128)}, u32[]{:S(2)}, u32[]{:S(2)}) async-start(s32[8,4,32,2048]{3,2,0,1:T(8,128)} %copy.23), calls=%async_computation.3 | async-start | bytes 16777216 | tf_op jit(solution)/shard_map/all_to_all | solution.py:49
